TPU v7x, 32 devices: a whole 2x2x4 slice. The times are simulated.
32 devices in a mesh: row: 8 (over z, y), col: 4 (over x, core).
Axes of the slice: x: 2, y: 2, z: 4, core: 2. Of those that a mesh axis runs over, the one named last changes fastest.
Arguments:
- matrix: float32 [4, 8, 512, 8, 4, 512], P(None, 'row', None, None, 'col'), may hold values from -30 to 30, as said below
Outputs:
- factored: float32 [4, 8, 512, 8, 4, 512], P(None, 'row', None, None, 'col')
Inputs may be any that keep to these rules, and one draw needn't show every extreme that they name: matrix is symmetric, positive definite and well conditioned.
All inputs are finite; a program needn't handle non-finite values.
Results may differ from a plain program's by a relative error of at most 0.00013.
Values sent between devices are 32-bit elements; how exact they have to be, the bound alone decides.
A program may use at most 192 MiB of HBM per device.

v0:
```python
import jax
import jax.numpy as jnp
from jax import lax
from jax.sharding import PartitionSpec as P

NB = 512
STEPS = 2


def spread(value, axis, source):
    kept = jnp.where(lax.axis_index(axis) == source, value, 0).astype(value.dtype)
    return lax.psum(kept, axis)


def trailing_product(column_panel, transposed):
    return jnp.einsum(
        "tan,sbn->tasb",
        column_panel,
        transposed,
        precision=lax.Precision.HIGHEST,
        preferred_element_type=jnp.float32,
    )


def shards(matrix):
    local_rows = matrix.shape[0]
    local_cols = matrix.shape[3]
    blocks = matrix.reshape(local_rows, NB, local_cols, NB)
    row_count = lax.axis_size("row")
    column_count = lax.axis_size("col")
    group_size = row_count // column_count
    row_place = lax.axis_index("row")
    column_place = lax.axis_index("col")
    tile_rows = jnp.arange(local_rows, dtype=jnp.int32) * row_count + row_place
    tile_columns = jnp.arange(local_cols, dtype=jnp.int32) * column_count + column_place
    anchor = jnp.int32(0)
    for step in range(STEPS):
        root_row = step % row_count
        factor_local_row = step // row_count
        root_col = step % column_count
        factor_local_col = step // column_count
        corner = blocks[factor_local_row, :, factor_local_col, :]
        owner = (row_place == root_row) & (column_place == root_col)
        identity = jnp.eye(NB, dtype=jnp.float32)
        chosen = jnp.where(owner, corner, identity)
        factor_local = jnp.linalg.cholesky(chosen)
        factor_diag_block = spread(factor_local, "row", root_row)
        source = blocks[:, :, factor_local_col, :]
        solved = jax.scipy.linalg.solve_triangular(
            factor_diag_block, source.reshape(local_rows * NB, NB).T, lower=True
        ).T
        solved = solved.reshape(local_rows, NB, NB)
        panel_local = jnp.where((tile_rows > step)[:, None, None], solved, 0.0)
        factor_column_panel = spread(panel_local, "col", root_col)
        empty = jnp.zeros((local_rows, group_size, NB, NB), jnp.float32)
        slot_index = row_place // column_count
        holder = row_place % column_count == column_place
        contribution = jnp.where(holder, factor_column_panel, 0.0)
        filled = lax.dynamic_update_slice(
            empty, contribution[:, None], (anchor, slot_index, anchor, anchor)
        )
        gathered = lax.psum(filled, "row")
        transposed = gathered.reshape(local_cols, NB, NB)
        diag_block, column_panel, transposed = (factor_diag_block, factor_column_panel, transposed)
        write_blocks = blocks
        local_row = step // row_count
        local_col = step // column_count
        column_now = write_blocks[:, :, local_col, :]
        owns_col = column_place == step % column_count
        row_after = (tile_rows > step)[:, None, None]
        row_hit = (tile_rows == step)[:, None, None]
        new_column = jnp.where(
            row_after, column_panel, jnp.where(row_hit, diag_block[None], column_now)
        )
        new_column = jnp.where(owns_col, new_column, column_now)
        write_blocks = write_blocks.at[:, :, local_col, :].set(new_column)
        row_now = write_blocks[local_row]
        owns_row = row_place == step % row_count
        zero_cols = (tile_columns > step)[None, :, None]
        new_row = jnp.where(owns_row & zero_cols, 0.0, row_now)
        blocks = write_blocks.at[local_row].set(new_row)
        blocks = blocks - trailing_product(column_panel, transposed)
    return blocks.reshape(matrix.shape)


def solution(mesh):
    in_specs = (P(None, "row", None, None, "col", None),)
    out_specs = P(None, "row", None, None, "col", None)
    return jax.shard_map(shards, mesh=mesh, in_specs=in_specs, out_specs=out_specs, check_vma=False)
```

profile of v0, /device:TPU:0, one launch (start us, length us, event | category | flops | bytes accessed | tf_op | source)
XLA Modules:
  0.0 1563.9 jit_solution(13661579687502120736)
XLA Ops:
  6.5 78.2 %copy.17 = f32[4,1,512,8,1,512]{2,5,3,0,4,1:T(8,128)} copy(f32[4,1,512,8,1,512]{5,4,3,2,1,0:T(1,128)} %param.12) | data formatting | bytes 67108864 | tf_op args[0]
  87.9 11.7 cholesky.286
  99.7 9.8 custom-call.27
  110.3 11.7 cholesky.305
  122.0 10.0 custom-call.28
  132.7 11.7 cholesky.326
  155.6 11.7 cholesky.343
  182.8 78.7 %copy.42 = f32[4,1,512,8,1,512]{2,5,0,3,1,4:T(8,128)} copy(f32[4,1,512,8,1,512]{5,4,3,2,1,0:T(1,128)} %param.12) | data formatting | bytes 67108864 | tf_op jit(solution)/shard_map/reshape | solution.py:28
  280.5 39.3 %custom-call.30 = f32[4,128,128]{1,2,0:T(8,128)S(1)} custom-call(f32[4,128,128]{2,1,0:T(8,128)S(1)} %get-tuple-element.69), custom_call_target="InvertDiagBlocksLowerTriangular" | custom-call | tf_op jit(solution)/shard_map/jit(_solve_triangular)/triangular_solve | solution.py:49
  355.9 88.4 %all-reduce.10.cloned.1.call-done = f32[4,512,512]{1,2,0:T(8,128)} async-done(((f32[4,512,512]{1,2,0:T(8,128)}), f32[4,512,512]{1,2,0:T(8,128)}) %all-reduce.10.cloned.1.call-update) | async-done | bytes 4194320 | tf_op jit(solution)/shard_map/psum | solution.py:12
  477.5 253.1 %all-reduce.12.cloned.1.call-done = f32[8,512,512]{2,1,0:T(8,128)} async-done(((f32[8,512,512]{2,1,0:T(8,128)}), f32[8,512,512]{2,1,0:T(8,128)}) %all-reduce.12.cloned.1.call-update) | async-done | bytes 8388624 | tf_op jit(solution)/shard_map/psum | solution.py:62
  730.6 63.0 %convolution_subtract_fusion = f32[4,512,8,512]{1,3,2,0:T(8,128)} fusion(f32[4,512,8,512]{1,3,2,0:T(8,128)} %fusion.1, f32[8,512,512]{2,1,0:T(8,128)} %all-reduce.12.cloned.1.call-done, f32[4,512,512]{1,2,0:T(8,128)} %all-reduce.10.cloned.1.call-done), kind=kOutput, calls=%fused_computation.5 | convolution fusion | flops 51547996160 | bytes 79691776 | tf_op jit(solution)/shard_map/tan,sbn->tasb/dot_general | solution.py:16
  796.7 11.7 cholesky.358
  808.6 9.8 custom-call.31
  819.1 11.7 cholesky.377
  832.2 10.2 custom-call.32
  843.0 11.7 cholesky.398
  865.9 11.7 cholesky.415
  894.3 65.6 %all-reduce.14.cloned.1.call-done = f32[512,512]{1,0:T(8,128)} async-done(((f32[512,512]{1,0:T(8,128)}), f32[512,512]{1,0:T(8,128)}) %all-reduce.14.cloned.1.call-update) | async-done | bytes 1048592 | tf_op jit(solution)/shard_map/psum | solution.py:12
  969.0 39.3 %custom-call.34 = f32[4,128,128]{1,2,0:T(8,128)S(1)} custom-call(f32[4,128,128]{2,1,0:T(8,128)S(1)} %get-tuple-element.70), custom_call_target="InvertDiagBlocksLowerTriangular" | custom-call | tf_op jit(solution)/shard_map/jit(_solve_triangular)/triangular_solve | solution.py:49
  1044.2 85.2 %all-reduce.16.cloned.1.call-done = f32[4,512,512]{1,2,0:T(8,128)} async-done(((f32[4,512,512]{1,2,0:T(8,128)}), f32[4,512,512]{1,2,0:T(8,128)}) %all-reduce.16.cloned.1.call-update) | async-done | bytes 4194320 | tf_op jit(solution)/shard_map/psum | solution.py:12
  1162.7 253.0 %all-reduce.18.cloned.1.call-done = f32[8,512,512]{2,1,0:T(8,128)} async-done(((f32[8,512,512]{2,1,0:T(8,128)}), f32[8,512,512]{2,1,0:T(8,128)}) %all-reduce.18.cloned.1.call-update) | async-done | bytes 8388624 | tf_op jit(solution)/shard_map/psum | solution.py:62
  1415.8 62.8 %subtract_bitcast_fusion = f32[4,1,512,8,1,512]{2,5,3,0,4,1:T(8,128)} fusion(f32[4,512,8,512]{1,3,2,0:T(8,128)} %fusion, f32[8,512,512]{2,1,0:T(8,128)} %all-reduce.18.cloned.1.call-done, f32[4,512,512]{1,2,0:T(8,128)} %all-reduce.16.cloned.1.call-done), kind=kOutput, calls=%fused_computation.4 | convolution fusion | flops 51547996160 | bytes 79691776 | tf_op jit(solution)/shard_map/tan,sbn->tasb/dot_general | solution.py:16
  1478.5 78.2 %copy.37 = f32[4,1,512,8,1,512]{5,4,3,2,1,0:T(1,128)} copy(f32[4,1,512,8,1,512]{2,5,3,0,4,1:T(8,128)} %subtract_bitcast_fusion) | data formatting | bytes 67108864 | tf_op jit(solution)/shard_map/reshape | solution.py:83
  (148 shorter events, 230.9 us)
Async XLA Ops:
  6.5 264.9 %all-reduce.8.cloned.1.call-start = ((), (), s32[]{:S(2)}) async-start(), calls=%async_computation | async-start | bytes 2097152 | tf_op jit(solution)/shard_map/psum | solution.py:12
  182.8 261.4 %all-reduce.10.cloned.1.call-start = ((), (), s32[]{:S(2)}) async-start(), calls=%async_computation.1 | async-start | bytes 8388608 | tf_op jit(solution)/shard_map/psum | solution.py:12
  319.8 6.6 copy-start.2
  355.8 374.8 %all-reduce.12.cloned.1.call-start = ((), (), s32[]{:S(2)}) async-start(), calls=%async_computation.2 | async-start | bytes 16777216 | tf_op jit(solution)/shard_map/psum | solution.py:62
  454.1 4.3 copy-start.1
  460.8 1.2 copy-start.4
  460.8 499.0 %all-reduce.14.cloned.1.call-start = ((), (), s32[]{:S(2)}) async-start(), calls=%async_computation.3 | async-start | bytes 2097152 | tf_op jit(solution)/shard_map/psum | solution.py:12
  882.2 247.2 %all-reduce.16.cloned.1.call-start = ((), (), s32[]{:S(2)}) async-start(), calls=%async_computation.4 | async-start | bytes 8388608 | tf_op jit(solution)/shard_map/psum | solution.py:12
  1008.4 6.6 copy-start.3
  1044.2 371.6 %all-reduce.18.cloned.1.call-start = ((), (), s32[]{:S(2)}) async-start(), calls=%async_computation.5 | async-start | bytes 16777216 | tf_op jit(solution)/shard_map/psum | solution.py:62
  1139.3 4.3 copy-start
  1146.0 1.2 copy-start.5
Sparse Core Ops, SparseCore 0:
  182.9 81.0 all-reduce.7
  355.9 88.2 all-reduce.9
  460.9 269.6 all-reduce.11
  882.3 77.4 all-reduce.13
  1044.3 85.0 all-reduce.15
  1146.1 269.5 all-reduce.17
where the time goes:
time: 1580 us; the launch traced here: 1560 us
  waiting for transfers between devices  745 us (47%)
  local copies, waits for them, and re-layouts  321 us (20%)
  other arithmetic  302 us (19%)
  matrix products  165 us (10%)
  between operations  30 us (2%)
    psum x2, waiting for transfers between devices, shards(): gathered = lax.psum(filled, 'row')  506 us
    psum x4, waiting for transfers between devices, spread(): return lax.psum(kept, axis)  239 us
    another operation x29, other arithmetic, shards(): factor_local = jnp.linalg.cholesky(chosen)  158 us
    dot_general x2, matrix products, trailing_product(): jnp.einsum('tan,sbn->tasb', column_panel, transposed, precision=lax.Preci...  126 us
    another operation x5, other arithmetic, shards(): jax.scipy.linalg.solve_triangular(factor_diag_block, source.reshape(local...  81.3 us
    unnamed x13, local copies, waits for them, and re-layouts  80.5 us
    reshape x1, local copies, waits for them, and re-layouts, shards(): blocks = matrix.reshape(local_rows, NB, local_cols, NB)  78.7 us
    reshape x1, local copies, waits for them, and re-layouts, shards(): return blocks.reshape(matrix.shape)  78.2 us
  transfers between devices with their start and end apart: 6, of which 5 were waited for; matrix products, arithmetic and copies ran while one was open for 8% of the time, Pallas kernels for 0%

commit v1 on v0

--- a/solution.py
+++ b/solution.py
@@ -9,7 +9,7 @@
 
 def spread(value, axis, source):
     kept = jnp.where(lax.axis_index(axis) == source, value, 0).astype(value.dtype)
-    return lax.psum(kept, axis)
+    return jnp.sum(lax.all_gather(kept, axis), axis=0)
 
 
 def trailing_product(column_panel, transposed):

time: 1580 us -> 1720 us (1.089)
  waiting for transfers between devices: 745 us -> 925 us
  local copies, waits for them, and re-layouts: 321 us -> 261 us
  other arithmetic: 302 us -> 330 us
    all_gather x0 -> x4, waiting for transfers between devices: none -> 428 us  [spread(): return jnp.sum(lax.all_gather(kept, axis), axis=0)]
    psum x4 -> x0, waiting for transfers between devices: 239 us -> none  [spread(): return lax.psum(kept, axis)]
    reshape x1 -> x0, local copies, waits for them, and re-layouts: 78.7 us -> none  [shards(): blocks = matrix.reshape(local_rows, NB, local_cols, NB)]
    reduce_sum x0 -> x4, other arithmetic: none -> 29.7 us  [spread(): return jnp.sum(lax.all_gather(kept, axis), axis=0)]
    unnamed x13 -> x11, local copies, waits for them, and re-layouts: 80.5 us -> 89.1 us
  transfers between devices with their start and end apart: 6 -> 6, of which waited for: 5 -> 6; matrix products, arithmetic and copies ran while one was open for 8% -> 4% of each run, Pallas kernels for 0% -> 0%
where the time goes in v1:
time: 1720 us; the launch traced here: 1700 us
  waiting for transfers between devices  925 us (54%)
  other arithmetic  330 us (19%)
  local copies, waits for them, and re-layouts  261 us (15%)
  matrix products  152 us (9%)
  between operations  32.8 us (2%)
    psum x2, waiting for transfers between devices, shards(): gathered = lax.psum(filled, 'row')  497 us
    all_gather x4, waiting for transfers between devices, spread(): return jnp.sum(lax.all_gather(kept, axis), axis=0)  428 us
    another operation x29, other arithmetic, shards(): factor_local = jnp.linalg.cholesky(chosen)  158 us
    dot_general x2, matrix products, trailing_product(): jnp.einsum('tan,sbn->tasb', column_panel, transposed, precision=lax.Preci...  126 us
    unnamed x11, local copies, waits for them, and re-layouts  89.1 us
    another operation x5, other arithmetic, shards(): jax.scipy.linalg.solve_triangular(factor_diag_block, source.reshape(local...  78.9 us
    reshape x1, local copies, waits for them, and re-layouts, shards(): return blocks.reshape(matrix.shape)  78.2 us
  transfers between devices with their start and end apart: 6, of which 6 were waited for; matrix products, arithmetic and copies ran while one was open for 4% of the time, Pallas kernels for 0%

profile of v1, /device:TPU:0, one launch (start us, length us, event | category | flops | bytes accessed | tf_op | source)
XLA Modules:
  0.0 1702.8 jit_solution(8540946298519223806)
XLA Ops:
  6.5 78.2 %copy.32 = f32[4,1,512,8,1,512]{2,5,3,0,4,1:T(8,128)} copy(f32[4,1,512,8,1,512]{5,4,3,2,1,0:T(1,128)} %param.12) | data formatting | bytes 67108864 | tf_op args[0]
  87.9 11.7 cholesky.286
  110.3 11.7 cholesky.305
  122.0 10.0 custom-call.28
  132.7 11.7 cholesky.326
  155.6 11.7 cholesky.343
  201.2 111.7 %all-gather.11.cloned.1.call-done = f32[4096,512]{1,0:T(8,128)} async-done(((f32[512,512]{1,0:T(8,128)}), f32[4096,512]{1,0:T(8,128)}) %all-gather.11.cloned.1.call-update) | async-done | bytes 8388624 | tf_op jit(solution)/shard_map/all_gather | solution.py:12
  325.8 39.3 %custom-call.30 = f32[4,128,128]{1,2,0:T(8,128)S(1)} custom-call(f32[4,128,128]{2,1,0:T(8,128)S(1)} %get-tuple-element.69), custom_call_target="InvertDiagBlocksLowerTriangular" | custom-call | tf_op jit(solution)/shard_map/jit(_solve_triangular)/triangular_solve | solution.py:49
  389.0 104.1 %all-gather.7.cloned.1.call-done = f32[4,4,512,512]{3,2,1,0:T(8,128)} async-done(((f32[1,4,512,512]{3,2,1,0:T(8,128)}), f32[4,4,512,512]{3,2,1,0:T(8,128)}) %all-gather.7.cloned.1.call-update) | async-done | bytes 16777232 | tf_op jit(solution)/shard_map/all_gather | solution.py:12
  493.2 10.4 reduce_sum.41
  547.5 248.6 %all-reduce.4.cloned.1.call-done = f32[8,512,512]{2,1,0:T(8,128)} async-done(((f32[8,512,512]{2,1,0:T(8,128)}), f32[8,512,512]{2,1,0:T(8,128)}) %all-reduce.4.cloned.1.call-update) | async-done | bytes 8388624 | tf_op jit(solution)/shard_map/psum | solution.py:62
  796.0 63.0 %convolution_subtract_fusion = f32[4,512,8,512]{1,3,2,0:T(8,128)} fusion(f32[4,512,8,512]{1,3,2,0:T(8,128)} %fusion.1, f32[8,512,512]{2,1,0:T(8,128)} %all-reduce.4.cloned.1.call-done, f32[4,512,512,1]{1,0,2,3:T(4,128)} %bitcast.153), kind=kOutput, calls=%fused_computation.5 | convolution fusion | flops 51547996160 | bytes 79691776 | tf_op jit(solution)/shard_map/tan,sbn->tasb/dot_general | solution.py:16
  862.1 11.7 cholesky.358
  884.5 11.7 cholesky.377
  897.6 10.2 custom-call.32
  908.5 11.7 cholesky.398
  931.3 11.7 cholesky.415
  963.1 108.2 %all-gather.13.cloned.1.call-done = f32[4096,512]{1,0:T(8,128)} async-done(((f32[512,512]{1,0:T(8,128)}), f32[4096,512]{1,0:T(8,128)}) %all-gather.13.cloned.1.call-update) | async-done | bytes 8388624 | tf_op jit(solution)/shard_map/all_gather | solution.py:12
  1084.1 39.3 %custom-call.34 = f32[4,128,128]{1,2,0:T(8,128)S(1)} custom-call(f32[4,128,128]{2,1,0:T(8,128)S(1)} %get-tuple-element.70), custom_call_target="InvertDiagBlocksLowerTriangular" | custom-call | tf_op jit(solution)/shard_map/jit(_solve_triangular)/triangular_solve | solution.py:49
  1147.6 104.0 %all-gather.9.cloned.1.call-done = f32[4,4,512,512]{3,2,1,0:T(8,128)} async-done(((f32[1,4,512,512]{3,2,1,0:T(8,128)}), f32[4,4,512,512]{3,2,1,0:T(8,128)}) %all-gather.9.cloned.1.call-update) | async-done | bytes 16777232 | tf_op jit(solution)/shard_map/all_gather | solution.py:12
  1251.5 10.3 reduce_sum.44
  1305.5 248.8 %all-reduce.6.cloned.1.call-done = f32[8,512,512]{2,1,0:T(8,128)} async-done(((f32[8,512,512]{2,1,0:T(8,128)}), f32[8,512,512]{2,1,0:T(8,128)}) %all-reduce.6.cloned.1.call-update) | async-done | bytes 8388624 | tf_op jit(solution)/shard_map/psum | solution.py:62
  1554.3 63.0 %subtract_bitcast_fusion = f32[4,1,512,8,1,512]{2,5,3,0,4,1:T(8,128)} fusion(f32[4,512,8,512]{1,3,2,0:T(8,128)} %fusion, f32[8,512,512]{2,1,0:T(8,128)} %all-reduce.6.cloned.1.call-done, f32[4,512,512,1]{1,0,2,3:T(4,128)} %bitcast.154), kind=kOutput, calls=%fused_computation.4 | convolution fusion | flops 51547996160 | bytes 79691776 | tf_op jit(solution)/shard_map/tan,sbn->tasb/dot_general | solution.py:16
  1617.3 78.2 %copy.53 = f32[4,1,512,8,1,512]{5,4,3,2,1,0:T(1,128)} copy(f32[4,1,512,8,1,512]{2,5,3,0,4,1:T(8,128)} %subtract_bitcast_fusion) | data formatting | bytes 67108864 | tf_op jit(solution)/shard_map/reshape | solution.py:83
  (151 shorter events, 265.1 us)
Async XLA Ops:
  6.5 306.4 %all-gather.11.cloned.1.call-start = ((), (), s32[]{:S(2)}) async-start(), calls=%async_computation.4 | async-start | bytes 9437184 | tf_op jit(solution)/shard_map/all_gather | solution.py:12
  185.6 307.6 %all-gather.7.cloned.1.call-start = ((), (), s32[]{:S(2)}) async-start(), calls=%async_computation | async-start | bytes 20971520 | tf_op jit(solution)/shard_map/all_gather | solution.py:12
  365.1 5.7 copy-start.2
  388.9 407.1 %all-reduce.4.cloned.1.call-start = ((), (), s32[]{:S(2)}) async-start(), calls=%async_computation.1 | async-start | bytes 16777216 | tf_op jit(solution)/shard_map/psum | solution.py:62
  519.3 4.3 copy-start.1
  526.0 545.3 %all-gather.13.cloned.1.call-start = ((), (), s32[]{:S(2)}) async-start(), calls=%async_computation.5 | async-start | bytes 9437184 | tf_op jit(solution)/shard_map/all_gather | solution.py:12
  947.6 303.9 %all-gather.9.cloned.1.call-start = ((), (), s32[]{:S(2)}) async-start(), calls=%async_computation.2 | async-start | bytes 20971520 | tf_op jit(solution)/shard_map/all_gather | solution.py:12
  1123.4 5.7 copy-start.3
  1147.3 407.0 %all-reduce.6.cloned.1.call-start = ((), (), s32[]{:S(2)}) async-start(), calls=%async_computation.3 | async-start | bytes 16777216 | tf_op jit(solution)/shard_map/psum | solution.py:62
  1277.6 4.3 copy-start
Sparse Core Ops, SparseCore 0:
  185.7 127.2 all-gather.10
  389.1 104.0 all-gather.6
  526.1 269.8 all-reduce.3
  947.7 123.5 all-gather.12
  1147.4 104.0 all-gather.8
  1284.4 269.8 all-reduce.5
